TPU v7x, 32 devices: a whole 2x2x4 slice. The times are simulated.
32 devices in a mesh: wide: 16 (over z, y, x), narrow: 2 (over core).
Axes of the slice: x: 2, y: 2, z: 4, core: 2. Of those that a mesh axis runs over, the one named last changes fastest.
Arguments:
- inputs: float32 [16, 64, 16, 128], P(None, 'wide', 'narrow'), may hold values from -100 to 100
- old_basis: float32 [256, 64, 16, 128], P(None, 'wide', 'narrow'), may hold values from -12 to 12
- conductance: float32 [64, 16, 128], P('wide', 'narrow'), may hold values from 0.5 to 2
- shifts: float32 [3], replicated, may hold values from 0.2 to 4
Outputs:
- new_columns: float32 [48, 64, 16, 128], P(None, 'wide', 'narrow')
- coefficients: float32 [256, 48], replicated
- col_scale: float32 [48], replicated
All inputs are finite; a program needn't handle non-finite values.
Results may differ from a plain program's by a relative error of at most 0.00011.
Values sent between devices are 32-bit elements; how exact they have to be, the bound alone decides.
No kernel may reach another device: no remote copies, remote signals or barrier semaphores. Data moves between devices by JAX's collectives and lax.ppermute only.
A program may use at most 64 MiB of HBM per device.

v0:
```python
import jax
import jax.numpy as jnp
from jax import lax
from jax.sharding import PartitionSpec as P

ITERS = 4


def padded_2(cells, sides, width):
    for axis, dim in sides:
        count = lax.axis_size(axis)
        ends = count - 1
        head = lax.slice_in_dim(cells, 0, width, axis=dim)
        tail = lax.slice_in_dim(cells, cells.shape[dim] - width, cells.shape[dim], axis=dim)
        cells = jnp.concatenate(
            [
                lax.ppermute(tail, axis, [(i, (i + 1) % count) for i in range(ends)]),
                cells,
                lax.ppermute(head, axis, [((i + 1) % count, i) for i in range(ends)]),
            ],
            axis=dim,
        )
    return cells


def spread(coef):
    return coef[:, None, None, None]


def stencil(padded, conductance, shift_col):
    center = padded[:, 1:-1, 1:-1, :]
    deeper = jnp.pad(padded, ((0, 0), (0, 0), (0, 0), (1, 1)))
    beside_all = deeper[:, 2:, 1:-1, 1:-1] + deeper[:, :-2, 1:-1, 1:-1]
    beside_all = beside_all + deeper[:, 1:-1, 2:, 1:-1] + deeper[:, 1:-1, :-2, 1:-1]
    beside_all = beside_all + deeper[:, 1:-1, 1:-1, 2:] + deeper[:, 1:-1, 1:-1, :-2]
    return conductance[None] * (6.0 * center - beside_all) + spread(shift_col) * center


def operate(values, conductance, shift_col):
    padded = padded_2(values, (("wide", 1), ("narrow", 2)), 1)
    return stencil(padded, conductance, shift_col)


def local_dot(left, right):
    return jnp.sum(left * right, axis=(1, 2, 3))


def shards(inputs, old_basis, conductance, shifts):
    total_cells = (
        inputs.shape[1]
        * inputs.shape[2]
        * inputs.shape[3]
        * lax.axis_size("wide")
        * lax.axis_size("narrow")
    )
    shift_col = jnp.repeat(shifts, inputs.shape[0])
    shadow = jnp.tile(inputs, (shifts.shape[0], 1, 1, 1))
    columns = shadow.shape[0]
    solution = jnp.zeros_like(shadow)
    residual = shadow
    search = shadow
    rho_now = lax.psum(local_dot(shadow, shadow), ("wide", "narrow")) / total_cells
    for iteration in range(ITERS):
        search_image = operate(search, conductance, shift_col)
        denominator = lax.psum(local_dot(shadow, search_image), ("wide", "narrow")) / total_cells
        step_alpha = rho_now / denominator
        halfway = residual - spread(step_alpha) * search_image
        halfway_image = operate(halfway, conductance, shift_col)
        cross_sum, square_sum, shadow_half, shadow_image = lax.psum(
            (
                local_dot(halfway_image, halfway),
                local_dot(halfway_image, halfway_image),
                local_dot(shadow, halfway),
                local_dot(shadow, halfway_image),
            ),
            ("wide", "narrow"),
        )
        step_omega = cross_sum / total_cells / (square_sum / total_cells + 1e-06)
        solution = solution + spread(step_alpha) * search + spread(step_omega) * halfway
        residual = halfway - spread(step_omega) * halfway_image
        rho_next = shadow_half / total_cells - step_omega * (shadow_image / total_cells)
        if iteration + 1 < ITERS:
            step_beta = rho_next / rho_now * (step_alpha / step_omega)
            search = residual + spread(step_beta) * (search - spread(step_omega) * search_image)
            rho_now = rho_next
    vflat = old_basis.reshape(old_basis.shape[0], -1)
    wflat = solution.reshape(columns, -1)
    high = lax.Precision.HIGHEST
    first_coef = (
        lax.psum(jnp.einsum("bc,kc->bk", vflat, wflat, precision=high), ("wide", "narrow"))
        / total_cells
    )
    once = wflat - jnp.einsum("bk,bc->kc", first_coef, vflat, precision=high)
    second_coef = (
        lax.psum(jnp.einsum("bc,kc->bk", vflat, once, precision=high), ("wide", "narrow"))
        / total_cells
    )
    twice = once - jnp.einsum("bk,bc->kc", second_coef, vflat, precision=high)
    mean_square = lax.psum(jnp.sum(twice * twice, axis=1), ("wide", "narrow")) / total_cells
    col_scale = jnp.sqrt(mean_square + 1e-06)
    new_columns = (twice / col_scale[:, None]).reshape(solution.shape)
    return (new_columns, first_coef + second_coef, col_scale)


def solution(mesh):
    in_specs = (
        P(None, "wide", "narrow", None),
        P(None, "wide", "narrow", None),
        P("wide", "narrow", None),
        P(),
    )
    out_specs = (P(None, "wide", "narrow", None), P(), P())
    return jax.shard_map(shards, mesh=mesh, in_specs=in_specs, out_specs=out_specs, check_vma=False)
```

profile of v0, /device:TPU:0, one launch (start us, length us, event | category | flops | bytes accessed | tf_op | source)
XLA Modules:
  0.0 634.8 jit_solution(9891462262970364943)
XLA Ops:
  1.9 4.9 collective-permute-start.1
  8.1 2.8 collective-permute-done.1
  10.9 6.2 collective-permute-done
  23.1 40.2 %all-reduce.12 = (f32[48]{0:T(128)S(1)}, f32[48]{0:T(128)S(1)}) all-reduce(f32[48]{0:T(128)S(1)} %get-tuple-element.50, f32[48]{0:T(128)S(1)} %reduce_sum.183), channel_id=1, replica_groups=mesh['wide'=16,'narrow'=2] {'wide','narrow'}, use_global_device_ids=true, to_apply=%region_3.4 | all-reduce | flops 96 | bytes 768 | tf_op jit(solution)/shard_map/psum | solution.py:65
  63.5 4.2 collective-permute-start.5
  69.0 6.1 collective-permute-done.5
  75.1 1.9 collective-permute-done.4
  79.6 2.0 collective-permute-done.6
  83.2 39.4 %all-reduce.11 = (f32[48]{0:T(128)S(1)}, f32[48]{0:T(128)S(1)}, f32[48]{0:T(128)S(1)}, f32[48]{0:T(128)S(1)}) all-reduce(f32[48]{0:T(128)S(1)} %get-tuple-element.4, f32[48]{0:T(128)S(1)} %get-tuple-element.6, f32[48]{0:T(128)S(1)} %get-tuple-element.5, ...), channel_id=1, replica_groups=mesh['wide'=16,'narrow'=2] {'wide','narrow'}, use_global_device_ids=true, to_apply=%region_5.6 | all-reduce | flops 192 | bytes 1536 | tf_op jit(solution)/shard_map/psum | solution.py:69
  122.9 4.2 collective-permute-start.9
  128.4 6.1 collective-permute-done.9
  134.5 1.9 collective-permute-done.8
  139.0 2.0 collective-permute-done.10
  142.4 38.4 %psum.160 = f32[48]{0:T(128)S(1)} all-reduce(f32[48]{0:T(128)S(1)} %get-tuple-element.44), channel_id=1, replica_groups=mesh['wide'=16,'narrow'=2] {'wide','narrow'}, use_global_device_ids=true, to_apply=%region_13.14 | all-reduce | flops 48 | bytes 384 | tf_op jit(solution)/shard_map/psum | solution.py:65
  182.2 4.2 collective-permute-start.13
  187.7 1.9 collective-permute-done.13
  189.5 5.9 collective-permute-done.12
  198.1 2.0 collective-permute-done.14
  200.9 1.6 fusion.32
  202.5 39.3 %all-reduce.10 = (f32[48]{0:T(128)S(1)}, f32[48]{0:T(128)S(1)}, f32[48]{0:T(128)S(1)}, f32[48]{0:T(128)S(1)}) all-reduce(f32[48]{0:T(128)S(1)} %get-tuple-element.14, f32[48]{0:T(128)S(1)} %get-tuple-element.16, f32[48]{0:T(128)S(1)} %get-tuple-element.15, ...), channel_id=1, replica_groups=mesh['wide'=16,'narrow'=2] {'wide','narrow'}, use_global_device_ids=true, to_apply=%region_15.16 | all-reduce | flops 192 | bytes 1536 | tf_op jit(solution)/shard_map/psum | solution.py:69
  243.3 4.2 collective-permute-start.17
  248.8 6.1 collective-permute-done.17
  254.9 1.9 collective-permute-done.16
  259.6 1.8 collective-permute-done.18
  263.6 38.4 %psum.165 = f32[48]{0:T(128)S(1)} all-reduce(f32[48]{0:T(128)S(1)} %get-tuple-element.38), channel_id=1, replica_groups=mesh['wide'=16,'narrow'=2] {'wide','narrow'}, use_global_device_ids=true, to_apply=%region_23.24 | all-reduce | flops 48 | bytes 384 | tf_op jit(solution)/shard_map/psum | solution.py:65
  303.6 4.2 collective-permute-start.21
  309.1 1.9 collective-permute-done.21
  310.9 5.9 collective-permute-done.20
  319.5 2.0 collective-permute-done.22
  323.9 39.3 %all-reduce.9 = (f32[48]{0:T(128)S(1)}, f32[48]{0:T(128)S(1)}, f32[48]{0:T(128)S(1)}, f32[48]{0:T(128)S(1)}) all-reduce(f32[48]{0:T(128)S(1)} %get-tuple-element.10, f32[48]{0:T(128)S(1)} %get-tuple-element.12, f32[48]{0:T(128)S(1)} %get-tuple-element.11, ...), channel_id=1, replica_groups=mesh['wide'=16,'narrow'=2] {'wide','narrow'}, use_global_device_ids=true, to_apply=%region_25.26 | all-reduce | flops 192 | bytes 1536 | tf_op jit(solution)/shard_map/psum | solution.py:69
  364.9 4.2 collective-permute-start.25
  370.4 6.1 collective-permute-done.25
  376.5 1.9 collective-permute-done.24
  381.0 2.0 collective-permute-done.26
  385.2 38.4 %psum.170 = f32[48]{0:T(128)S(1)} all-reduce(f32[48]{0:T(128)S(1)} %get-tuple-element.33), channel_id=1, replica_groups=mesh['wide'=16,'narrow'=2] {'wide','narrow'}, use_global_device_ids=true, to_apply=%region_33.34 | all-reduce | flops 48 | bytes 384 | tf_op jit(solution)/shard_map/psum | solution.py:65
  425.2 4.2 collective-permute-start.29
  430.7 1.9 collective-permute-done.29
  432.6 5.9 collective-permute-done.28
  441.1 2.0 collective-permute-done.30
  444.5 39.3 %all-reduce.8 = (f32[48]{0:T(128)S(1)}, f32[48]{0:T(128)S(1)}) all-reduce(f32[48]{0:T(128)S(1)} %get-tuple-element.8, f32[48]{0:T(128)S(1)} %get-tuple-element.7), channel_id=1, replica_groups=mesh['wide'=16,'narrow'=2] {'wide','narrow'}, use_global_device_ids=true, to_apply=%region_37.38 | all-reduce | flops 96 | bytes 768 | tf_op jit(solution)/shard_map/psum | solution.py:69
  483.8 2.3 fusion.26
  486.7 5.3 fusion.10
  492.0 40.2 %psum.173 = f32[256,48]{0,1:T(8,128)S(1)} all-reduce(f32[256,48]{0,1:T(8,128)S(1)} %fusion.10), channel_id=1, replica_groups=mesh['wide'=16,'narrow'=2] {'wide','narrow'}, use_global_device_ids=true, to_apply=%region_38.39 | all-reduce | flops 12288 | bytes 98304 | tf_op jit(solution)/shard_map/psum | solution.py:90
  532.2 7.3 %convolution_subtract_fusion.1 = f32[48,4096]{1,0:T(8,128)S(1)} fusion(f32[32,8,32,128]{3,2,1,0:T(8,128)} %bitcast.104, f32[6,8,32,128]{3,2,1,0:T(8,128)S(1)} %bitcast.111, f32[256,48]{0,1:T(8,128)S(1)} %psum.173), kind=kOutput, calls=%fused_computation.16 | convolution fusion | flops 604188672 | bytes 5816320 | tf_op jit(solution)/shard_map/bk,bc->kc/dot_general | solution.py:93
  539.6 5.3 fusion.13
  544.9 41.0 %psum.174 = f32[256,48]{0,1:T(8,128)S(1)} all-reduce(f32[256,48]{0,1:T(8,128)S(1)} %fusion.13), channel_id=1, replica_groups=mesh['wide'=16,'narrow'=2] {'wide','narrow'}, use_global_device_ids=true, to_apply=%region_39.40 | all-reduce | flops 12288 | bytes 98304 | tf_op jit(solution)/shard_map/psum | solution.py:95
  586.6 7.0 %multiply_reduce_fusion = (f32[48]{0:T(128)S(1)}, f32[48,4096]{1,0:T(8,128)S(1)}) fusion(f32[48,4096]{1,0:T(8,128)S(1)} %convolution_subtract_fusion.1, f32[32,8,32,128]{3,2,1,0:T(8,128)} %bitcast.105, f32[256,48]{0,1:T(8,128)S(1)} %psum.174), kind=kOutput, calls=%fused_computation.211 | convolution fusion | flops 604581824 | bytes 5816512 | tf_op jit(solution)/shard_map/bk,bc->kc/dot_general | solution.py:98
  593.6 39.6 %psum.175 = f32[48]{0:T(128)S(1)} all-reduce(f32[48]{0:T(128)S(1)} %get-tuple-element.84), channel_id=1, replica_groups=mesh['wide'=16,'narrow'=2] {'wide','narrow'}, use_global_device_ids=true, to_apply=%region_41.42 | all-reduce | flops 48 | bytes 384 | tf_op jit(solution)/shard_map/psum | solution.py:99
  (111 shorter events, 58.7 us)
Async XLA Ops:
  0.6 19.1 %copy-start.6 = (f32[16,4,8,128]{3,2,1,0:T(8,128)S(1)}, f32[16,4,8,128]{3,2,1,0:T(8,128)}, u32[]{:S(2)}) copy-start(f32[16,4,8,128]{3,2,1,0:T(8,128)} %param.4) | copy-start | bytes 786436
  0.6 19.2 %copy-start.9 = (f32[3]{0:T(128)S(1)}, f32[3]{0:T(128)}, u32[]{:S(2)}) copy-start(f32[3]{0:T(128)} %param.7) | copy-start | bytes 40
  1.9 9.0 %collective-permute-start.1 = (f32[48,1,8,128]{3,0,2,1:T(8,128)S(1)}, f32[48,1,8,128]{3,0,2,1:T(8,128)S(1)}, u32[]{:S(2)}, u32[]{:S(2)}) collective-permute-start(f32[48,1,8,128]{3,0,2,1:T(8,128)S(1)} %get-tuple-element.82), channel_id=1, source_target_pairs={{0,2},{2,4},{4,6},{6,8},{8,10},{10,12},{12,14},{14,16},{16,18},{18... | collective-permute-start | bytes 589832 | tf_op jit(solution)/shard_map/ppermute | solution.py:17
  6.8 10.3 %collective-permute-start = (f32[48,1,8,128]{3,0,2,1:T(8,128)S(1)}, f32[48,1,8,128]{3,0,2,1:T(8,128)S(1)}, u32[]{:S(2)}, u32[]{:S(2)}) collective-permute-start(f32[48,1,8,128]{3,0,2,1:T(8,128)S(1)} %get-tuple-element.83), channel_id=1, source_target_pairs={{2,0},{4,2},{6,4},{8,6},{10,8},{12,10},{14,12},{16,14},{18,16},{20... | collective-permute-start | bytes 589832 | tf_op jit(solution)/shard_map/ppermute | solution.py:19
  17.1 5.4 copy-start.7
  17.1 3.1 collective-permute-start.3
  18.4 3.3 collective-permute-start.2
  23.1 157.7 %copy-start.2 = (f32[48,4,8,128]{3,0,2,1:T(8,128)}, f32[48,4,8,128]{3,0,2,1:T(8,128)S(1)}, u32[]{:S(2)}) copy-start(f32[48,4,8,128]{3,0,2,1:T(8,128)S(1)} %get-tuple-element.51) | copy-start | bytes 2359300
  63.5 11.6 %collective-permute-start.5 = (f32[48,1,8,128]{3,0,2,1:T(8,128)S(1)}, f32[48,1,8,128]{3,0,2,1:T(8,128)S(1)}, u32[]{:S(2)}, u32[]{:S(2)}) collective-permute-start(f32[48,1,8,128]{3,0,2,1:T(8,128)S(1)} %get-tuple-element.80), channel_id=1, source_target_pairs={{0,2},{2,4},{4,6},{6,8},{8,10},{10,12},{12,14},{14,16},{16,18},{18... | collective-permute-start | bytes 589832 | tf_op jit(solution)/shard_map/ppermute | solution.py:17
  67.7 9.3 %collective-permute-start.4 = (f32[48,1,8,128]{3,0,2,1:T(8,128)S(1)}, f32[48,1,8,128]{3,0,2,1:T(8,128)S(1)}, u32[]{:S(2)}, u32[]{:S(2)}) collective-permute-start(f32[48,1,8,128]{3,0,2,1:T(8,128)S(1)} %get-tuple-element.81), channel_id=1, source_target_pairs={{2,0},{4,2},{6,4},{8,6},{10,8},{12,10},{14,12},{16,14},{18,16},{20... | collective-permute-start | bytes 589832 | tf_op jit(solution)/shard_map/ppermute | solution.py:19
  77.0 2.6 collective-permute-start.7
  78.3 3.3 collective-permute-start.6
  83.2 58.6 %copy-start.5 = (f32[48,4,8,128]{3,0,2,1:T(8,128)}, f32[48,4,8,128]{3,0,2,1:T(8,128)S(1)}, u32[]{:S(2)}) copy-start(f32[48,4,8,128]{3,0,2,1:T(8,128)S(1)} %get-tuple-element.49) | copy-start | bytes 2359300
  122.9 11.6 %collective-permute-start.9 = (f32[48,1,8,128]{3,0,2,1:T(8,128)S(1)}, f32[48,1,8,128]{3,0,2,1:T(8,128)S(1)}, u32[]{:S(2)}, u32[]{:S(2)}) collective-permute-start(f32[48,1,8,128]{3,0,2,1:T(8,128)S(1)} %get-tuple-element.78), channel_id=1, source_target_pairs={{0,2},{2,4},{4,6},{6,8},{8,10},{10,12},{12,14},{14,16},{16,18},{18... | collective-permute-start | bytes 589832 | tf_op jit(solution)/shard_map/ppermute | solution.py:17
  127.1 9.3 %collective-permute-start.8 = (f32[48,1,8,128]{3,0,2,1:T(8,128)S(1)}, f32[48,1,8,128]{3,0,2,1:T(8,128)S(1)}, u32[]{:S(2)}, u32[]{:S(2)}) collective-permute-start(f32[48,1,8,128]{3,0,2,1:T(8,128)S(1)} %get-tuple-element.79), channel_id=1, source_target_pairs={{2,0},{4,2},{6,4},{8,6},{10,8},{12,10},{14,12},{16,14},{18,16},{20... | collective-permute-start | bytes 589832 | tf_op jit(solution)/shard_map/ppermute | solution.py:19
  136.4 2.6 collective-permute-start.11
  137.7 3.3 collective-permute-start.10
  182.2 7.4 %collective-permute-start.13 = (f32[48,1,8,128]{3,0,2,1:T(8,128)S(1)}, f32[48,1,8,128]{3,0,2,1:T(8,128)S(1)}, u32[]{:S(2)}, u32[]{:S(2)}) collective-permute-start(f32[48,1,8,128]{3,0,2,1:T(8,128)S(1)} %get-tuple-element.76), channel_id=1, source_target_pairs={{0,2},{2,4},{4,6},{6,8},{8,10},{10,12},{12,14},{14,16},{16,18},{18... | collective-permute-start | bytes 589832 | tf_op jit(solution)/shard_map/ppermute | solution.py:17
  186.4 9.1 %collective-permute-start.12 = (f32[48,1,8,128]{3,0,2,1:T(8,128)S(1)}, f32[48,1,8,128]{3,0,2,1:T(8,128)S(1)}, u32[]{:S(2)}, u32[]{:S(2)}) collective-permute-start(f32[48,1,8,128]{3,0,2,1:T(8,128)S(1)} %get-tuple-element.77), channel_id=1, source_target_pairs={{2,0},{4,2},{6,4},{8,6},{10,8},{12,10},{14,12},{16,14},{18,16},{20... | collective-permute-start | bytes 589832 | tf_op jit(solution)/shard_map/ppermute | solution.py:19
  195.5 2.6 collective-permute-start.15
  196.8 3.3 collective-permute-start.14
  243.3 11.6 %collective-permute-start.17 = (f32[48,1,8,128]{3,0,2,1:T(8,128)S(1)}, f32[48,1,8,128]{3,0,2,1:T(8,128)S(1)}, u32[]{:S(2)}, u32[]{:S(2)}) collective-permute-start(f32[48,1,8,128]{3,0,2,1:T(8,128)S(1)} %get-tuple-element.74), channel_id=1, source_target_pairs={{0,2},{2,4},{4,6},{6,8},{8,10},{10,12},{12,14},{14,16},{16,18},{18... | collective-permute-start | bytes 589832 | tf_op jit(solution)/shard_map/ppermute | solution.py:17
  247.5 9.3 %collective-permute-start.16 = (f32[48,1,8,128]{3,0,2,1:T(8,128)S(1)}, f32[48,1,8,128]{3,0,2,1:T(8,128)S(1)}, u32[]{:S(2)}, u32[]{:S(2)}) collective-permute-start(f32[48,1,8,128]{3,0,2,1:T(8,128)S(1)} %get-tuple-element.75), channel_id=1, source_target_pairs={{2,0},{4,2},{6,4},{8,6},{10,8},{12,10},{14,12},{16,14},{18,16},{20... | collective-permute-start | bytes 589832 | tf_op jit(solution)/shard_map/ppermute | solution.py:19
  256.8 2.8 collective-permute-start.19
  258.1 3.3 collective-permute-start.18
  303.6 7.4 %collective-permute-start.21 = (f32[48,1,8,128]{3,0,2,1:T(8,128)S(1)}, f32[48,1,8,128]{3,0,2,1:T(8,128)S(1)}, u32[]{:S(2)}, u32[]{:S(2)}) collective-permute-start(f32[48,1,8,128]{3,0,2,1:T(8,128)S(1)} %get-tuple-element.72), channel_id=1, source_target_pairs={{0,2},{2,4},{4,6},{6,8},{8,10},{10,12},{12,14},{14,16},{16,18},{18... | collective-permute-start | bytes 589832 | tf_op jit(solution)/shard_map/ppermute | solution.py:17
  307.8 9.1 %collective-permute-start.20 = (f32[48,1,8,128]{3,0,2,1:T(8,128)S(1)}, f32[48,1,8,128]{3,0,2,1:T(8,128)S(1)}, u32[]{:S(2)}, u32[]{:S(2)}) collective-permute-start(f32[48,1,8,128]{3,0,2,1:T(8,128)S(1)} %get-tuple-element.73), channel_id=1, source_target_pairs={{2,0},{4,2},{6,4},{8,6},{10,8},{12,10},{14,12},{16,14},{18,16},{20... | collective-permute-start | bytes 589832 | tf_op jit(solution)/shard_map/ppermute | solution.py:19
  316.9 2.6 collective-permute-start.23
  318.2 3.3 collective-permute-start.22
  364.9 19.0 %copy-start.3 = (f32[48,4,8,128]{3,0,2,1:T(8,128)}, f32[48,4,8,128]{3,0,2,1:T(8,128)S(1)}, u32[]{:S(2)}) copy-start(f32[48,4,8,128]{3,0,2,1:T(8,128)S(1)} %multiply_add_fusion) | copy-start | bytes 2359300
  364.9 11.6 %collective-permute-start.25 = (f32[48,1,8,128]{3,0,2,1:T(8,128)S(1)}, f32[48,1,8,128]{3,0,2,1:T(8,128)S(1)}, u32[]{:S(2)}, u32[]{:S(2)}) collective-permute-start(f32[48,1,8,128]{3,0,2,1:T(8,128)S(1)} %get-tuple-element.70), channel_id=1, source_target_pairs={{0,2},{2,4},{4,6},{6,8},{8,10},{10,12},{12,14},{14,16},{16,18},{18... | collective-permute-start | bytes 589832 | tf_op jit(solution)/shard_map/ppermute | solution.py:17
  369.1 9.3 %collective-permute-start.24 = (f32[48,1,8,128]{3,0,2,1:T(8,128)S(1)}, f32[48,1,8,128]{3,0,2,1:T(8,128)S(1)}, u32[]{:S(2)}, u32[]{:S(2)}) collective-permute-start(f32[48,1,8,128]{3,0,2,1:T(8,128)S(1)} %get-tuple-element.71), channel_id=1, source_target_pairs={{2,0},{4,2},{6,4},{8,6},{10,8},{12,10},{14,12},{16,14},{18,16},{20... | collective-permute-start | bytes 589832 | tf_op jit(solution)/shard_map/ppermute | solution.py:19
  378.4 2.6 collective-permute-start.27
  379.7 3.3 collective-permute-start.26
  425.2 18.8 %copy-start.4 = (f32[48,4,8,128]{3,0,2,1:T(8,128)}, f32[48,4,8,128]{3,0,2,1:T(8,128)S(1)}, u32[]{:S(2)}) copy-start(f32[48,4,8,128]{3,0,2,1:T(8,128)S(1)} %multiply_subtract_fusion) | copy-start | bytes 2359300
  425.2 7.4 %collective-permute-start.29 = (f32[48,1,8,128]{3,0,2,1:T(8,128)S(1)}, f32[48,1,8,128]{3,0,2,1:T(8,128)S(1)}, u32[]{:S(2)}, u32[]{:S(2)}) collective-permute-start(f32[48,1,8,128]{3,0,2,1:T(8,128)S(1)} %get-tuple-element.68), channel_id=1, source_target_pairs={{0,2},{2,4},{4,6},{6,8},{8,10},{10,12},{12,14},{14,16},{16,18},{18... | collective-permute-start | bytes 589832 | tf_op jit(solution)/shard_map/ppermute | solution.py:17
  429.4 9.1 %collective-permute-start.28 = (f32[48,1,8,128]{3,0,2,1:T(8,128)S(1)}, f32[48,1,8,128]{3,0,2,1:T(8,128)S(1)}, u32[]{:S(2)}, u32[]{:S(2)}) collective-permute-start(f32[48,1,8,128]{3,0,2,1:T(8,128)S(1)} %get-tuple-element.69), channel_id=1, source_target_pairs={{2,0},{4,2},{6,4},{8,6},{10,8},{12,10},{14,12},{16,14},{18,16},{20... | collective-permute-start | bytes 589832 | tf_op jit(solution)/shard_map/ppermute | solution.py:19
  438.5 2.6 collective-permute-start.31
  439.8 3.3 collective-permute-start.30
  483.8 2.9 copy-start
  532.2 7.3 %copy-start.1 = (f32[256,4,8,128]{3,2,1,0:T(8,128)S(1)}, f32[256,4,8,128]{3,2,1,0:T(8,128)}, u32[]{:S(2)}) copy-start(f32[256,4,8,128]{3,2,1,0:T(8,128)} %param.5) | copy-start | bytes 12582916
  633.2 1.2 copy-start.8
where the time goes:
time: 646 us; the launch traced here: 635 us
  blocking collectives  433 us (67%)
  waiting for transfers between devices  79.2 us (12%)
  starting transfers between devices  65.5 us (10%)
  other arithmetic  26.5 us (4%)
  matrix products  25 us (4%)
    psum x4, blocking collectives, shards(): lax.psum((local_dot(halfway_image, halfway), local_dot(halfway_image, hal...  157 us
    psum x4, blocking collectives, shards(): lax.psum(local_dot(shadow, search_image), ('wide', 'narrow')) / total_cells  155 us
    ppermute x16, waiting for transfers between devices, padded_2(): lax.ppermute(head, axis, [((i + 1) % count, i) for i in range(ends)])  46.5 us
    ppermute x16, starting transfers between devices, padded_2(): lax.ppermute(tail, axis, [(i, (i + 1) % count) for i in range(ends)])  44.6 us
    psum x1, blocking collectives, shards(): lax.psum(jnp.einsum('bc,kc->bk', vflat, once, precision=high), ('wide', '...  41 us
    psum x1, blocking collectives, shards(): lax.psum(jnp.einsum('bc,kc->bk', vflat, wflat, precision=high), ('wide',...  40.2 us
    psum x1, blocking collectives, shards(): lax.psum(jnp.sum(twice * twice, axis=1), ('wide', 'narrow')) / total_cells  39.6 us
    ppermute x16, waiting for transfers between devices, padded_2(): lax.ppermute(tail, axis, [(i, (i + 1) % count) for i in range(ends)])  32.8 us
  transfers between devices with their start and end apart: 32, of which 24 were waited for; matrix products, arithmetic and copies ran while one was open for 0% of the time, Pallas kernels for 0%

commit v1 on v0

--- a/solution.py
+++ b/solution.py
@@ -87,7 +87,7 @@
     wflat = solution.reshape(columns, -1)
     high = lax.Precision.HIGHEST
     first_coef = (
-        lax.psum(jnp.einsum("bc,kc->bk", vflat, wflat, precision=high), ("wide", "narrow"))
+        lax.psum(lax.psum(jnp.einsum("bc,kc->bk", vflat, wflat, precision=high), "wide"), "narrow")
         / total_cells
     )
     once = wflat - jnp.einsum("bk,bc->kc", first_coef, vflat, precision=high)

time: 646 us -> 684 us (1.059)
  blocking collectives: 433 us -> 472 us
    psum x1 -> x2, blocking collectives: 40.2 us -> 80.3 us  [the longest x1 76.5 us: shards(): lax.psum(jnp.einsum('bc,kc->bk', vflat, wflat, precision=high), 'wide')]
where the time goes in v1:
time: 684 us; the launch traced here: 673 us
  blocking collectives  472 us (69%)
  waiting for transfers between devices  79.2 us (12%)
  starting transfers between devices  65.5 us (10%)
  other arithmetic  26.5 us (4%)
  matrix products  25 us (4%)
    psum x4, blocking collectives, shards(): lax.psum((local_dot(halfway_image, halfway), local_dot(halfway_image, hal...  157 us
    psum x4, blocking collectives, shards(): lax.psum(local_dot(shadow, search_image), ('wide', 'narrow')) / total_cells  155 us
    psum x1, blocking collectives, shards(): lax.psum(jnp.einsum('bc,kc->bk', vflat, wflat, precision=high), 'wide')  76.5 us
    ppermute x16, waiting for transfers between devices, padded_2(): lax.ppermute(head, axis, [((i + 1) % count, i) for i in range(ends)])  46.5 us
    ppermute x16, starting transfers between devices, padded_2(): lax.ppermute(tail, axis, [(i, (i + 1) % count) for i in range(ends)])  44.6 us
    psum x1, blocking collectives, shards(): lax.psum(jnp.sum(twice * twice, axis=1), ('wide', 'narrow')) / total_cells  41.1 us
    psum x1, blocking collectives, shards(): lax.psum(jnp.einsum('bc,kc->bk', vflat, once, precision=high), ('wide', '...  37.5 us
    ppermute x16, waiting for transfers between devices, padded_2(): lax.ppermute(tail, axis, [(i, (i + 1) % count) for i in range(ends)])  32.7 us
  transfers between devices with their start and end apart: 32, of which 24 were waited for; matrix products, arithmetic and copies ran while one was open for 0% of the time, Pallas kernels for 0%

profile of v1, /device:TPU:0, one launch (start us, length us, event | category | flops | bytes accessed | tf_op | source)
XLA Modules:
  0.0 673.2 jit_solution(4275067333739099576)
XLA Ops:
  1.9 4.9 collective-permute-start.1
  8.1 2.8 collective-permute-done.1
  10.9 6.2 collective-permute-done
  23.1 40.2 %all-reduce.12 = (f32[48]{0:T(128)S(1)}, f32[48]{0:T(128)S(1)}) all-reduce(f32[48]{0:T(128)S(1)} %get-tuple-element.50, f32[48]{0:T(128)S(1)} %reduce_sum.183), channel_id=1, replica_groups=mesh['wide'=16,'narrow'=2] {'wide','narrow'}, use_global_device_ids=true, to_apply=%region_3.4 | all-reduce | flops 96 | bytes 768 | tf_op jit(solution)/shard_map/psum | solution.py:65
  63.5 4.2 collective-permute-start.5
  69.0 6.1 collective-permute-done.5
  75.1 1.9 collective-permute-done.4
  79.6 2.0 collective-permute-done.6
  83.2 39.4 %all-reduce.11 = (f32[48]{0:T(128)S(1)}, f32[48]{0:T(128)S(1)}, f32[48]{0:T(128)S(1)}, f32[48]{0:T(128)S(1)}) all-reduce(f32[48]{0:T(128)S(1)} %get-tuple-element.4, f32[48]{0:T(128)S(1)} %get-tuple-element.6, f32[48]{0:T(128)S(1)} %get-tuple-element.5, ...), channel_id=1, replica_groups=mesh['wide'=16,'narrow'=2] {'wide','narrow'}, use_global_device_ids=true, to_apply=%region_5.6 | all-reduce | flops 192 | bytes 1536 | tf_op jit(solution)/shard_map/psum | solution.py:69
  122.9 4.2 collective-permute-start.9
  128.4 6.1 collective-permute-done.9
  134.5 1.9 collective-permute-done.8
  139.0 2.0 collective-permute-done.10
  142.4 38.4 %psum.167 = f32[48]{0:T(128)S(1)} all-reduce(f32[48]{0:T(128)S(1)} %get-tuple-element.44), channel_id=1, replica_groups=mesh['wide'=16,'narrow'=2] {'wide','narrow'}, use_global_device_ids=true, to_apply=%region_13.14 | all-reduce | flops 48 | bytes 384 | tf_op jit(solution)/shard_map/psum | solution.py:65
  182.2 4.2 collective-permute-start.13
  187.7 1.9 collective-permute-done.13
  189.5 5.9 collective-permute-done.12
  198.1 2.0 collective-permute-done.14
  202.5 39.3 %all-reduce.10 = (f32[48]{0:T(128)S(1)}, f32[48]{0:T(128)S(1)}, f32[48]{0:T(128)S(1)}, f32[48]{0:T(128)S(1)}) all-reduce(f32[48]{0:T(128)S(1)} %get-tuple-element.14, f32[48]{0:T(128)S(1)} %get-tuple-element.16, f32[48]{0:T(128)S(1)} %get-tuple-element.15, ...), channel_id=1, replica_groups=mesh['wide'=16,'narrow'=2] {'wide','narrow'}, use_global_device_ids=true, to_apply=%region_15.16 | all-reduce | flops 192 | bytes 1536 | tf_op jit(solution)/shard_map/psum | solution.py:69
  243.3 4.2 collective-permute-start.17
  248.8 6.1 collective-permute-done.17
  254.9 1.9 collective-permute-done.16
  259.6 1.8 collective-permute-done.18
  263.6 38.4 %psum.172 = f32[48]{0:T(128)S(1)} all-reduce(f32[48]{0:T(128)S(1)} %get-tuple-element.38), channel_id=1, replica_groups=mesh['wide'=16,'narrow'=2] {'wide','narrow'}, use_global_device_ids=true, to_apply=%region_23.24 | all-reduce | flops 48 | bytes 384 | tf_op jit(solution)/shard_map/psum | solution.py:65
  303.6 4.2 collective-permute-start.21
  309.1 1.9 collective-permute-done.21
  310.9 5.9 collective-permute-done.20
  319.5 2.0 collective-permute-done.22
  323.9 39.3 %all-reduce.9 = (f32[48]{0:T(128)S(1)}, f32[48]{0:T(128)S(1)}, f32[48]{0:T(128)S(1)}, f32[48]{0:T(128)S(1)}) all-reduce(f32[48]{0:T(128)S(1)} %get-tuple-element.10, f32[48]{0:T(128)S(1)} %get-tuple-element.12, f32[48]{0:T(128)S(1)} %get-tuple-element.11, ...), channel_id=1, replica_groups=mesh['wide'=16,'narrow'=2] {'wide','narrow'}, use_global_device_ids=true, to_apply=%region_25.26 | all-reduce | flops 192 | bytes 1536 | tf_op jit(solution)/shard_map/psum | solution.py:69
  364.9 4.2 collective-permute-start.25
  370.4 6.1 collective-permute-done.25
  376.5 1.9 collective-permute-done.24
  381.0 2.0 collective-permute-done.26
  385.2 38.4 %psum.177 = f32[48]{0:T(128)S(1)} all-reduce(f32[48]{0:T(128)S(1)} %get-tuple-element.33), channel_id=1, replica_groups=mesh['wide'=16,'narrow'=2] {'wide','narrow'}, use_global_device_ids=true, to_apply=%region_33.34 | all-reduce | flops 48 | bytes 384 | tf_op jit(solution)/shard_map/psum | solution.py:65
  425.2 4.2 collective-permute-start.29
  430.7 1.9 collective-permute-done.29
  432.6 5.9 collective-permute-done.28
  441.1 2.0 collective-permute-done.30
  444.5 39.5 %all-reduce.8 = (f32[48]{0:T(128)S(1)}, f32[48]{0:T(128)S(1)}) all-reduce(f32[48]{0:T(128)S(1)} %get-tuple-element.8, f32[48]{0:T(128)S(1)} %get-tuple-element.7), channel_id=1, replica_groups=mesh['wide'=16,'narrow'=2] {'wide','narrow'}, use_global_device_ids=true, to_apply=%region_37.38 | all-reduce | flops 96 | bytes 768 | tf_op jit(solution)/shard_map/psum | solution.py:69
  484.0 2.3 fusion.26
  486.9 5.3 fusion.10
  492.2 76.5 %psum.180 = f32[256,48]{0,1:T(8,128)S(1)} all-reduce(f32[256,48]{0,1:T(8,128)S(1)} %fusion.10), channel_id=1, replica_groups=mesh['wide'=16,'narrow'=2] {'wide'}, use_global_device_ids=true, to_apply=%region_38.39 | all-reduce | flops 12288 | bytes 98304 | tf_op jit(solution)/shard_map/psum | solution.py:90
  568.7 3.8 psum.181
  572.5 7.3 %convolution_subtract_fusion.1 = f32[48,4096]{1,0:T(8,128)S(1)} fusion(f32[32,8,32,128]{3,2,1,0:T(8,128)} %bitcast.104, f32[6,8,32,128]{3,2,1,0:T(8,128)S(1)} %bitcast.111, f32[256,48]{0,1:T(8,128)S(1)} %psum.181), kind=kOutput, calls=%fused_computation.16 | convolution fusion | flops 604188672 | bytes 5816320 | tf_op jit(solution)/shard_map/bk,bc->kc/dot_general | solution.py:93
  579.8 5.3 fusion.13
  585.2 37.5 %psum.182 = f32[256,48]{0,1:T(8,128)S(1)} all-reduce(f32[256,48]{0,1:T(8,128)S(1)} %fusion.13), channel_id=1, replica_groups=mesh['wide'=16,'narrow'=2] {'wide','narrow'}, use_global_device_ids=true, to_apply=%region_40.41 | all-reduce | flops 12288 | bytes 98304 | tf_op jit(solution)/shard_map/psum | solution.py:95
  623.4 7.0 %multiply_reduce_fusion = (f32[48]{0:T(128)S(1)}, f32[48,4096]{1,0:T(8,128)S(1)}) fusion(f32[48,4096]{1,0:T(8,128)S(1)} %convolution_subtract_fusion.1, f32[32,8,32,128]{3,2,1,0:T(8,128)} %bitcast.105, f32[256,48]{0,1:T(8,128)S(1)} %psum.182), kind=kOutput, calls=%fused_computation.211 | convolution fusion | flops 604581824 | bytes 5816512 | tf_op jit(solution)/shard_map/bk,bc->kc/dot_general | solution.py:98
  630.4 41.1 %psum.183 = f32[48]{0:T(128)S(1)} all-reduce(f32[48]{0:T(128)S(1)} %get-tuple-element.84), channel_id=1, replica_groups=mesh['wide'=16,'narrow'=2] {'wide','narrow'}, use_global_device_ids=true, to_apply=%region_42.43 | all-reduce | flops 48 | bytes 384 | tf_op jit(solution)/shard_map/psum | solution.py:99
  (112 shorter events, 60.3 us)
Async XLA Ops:
  0.6 19.1 %copy-start.6 = (f32[16,4,8,128]{3,2,1,0:T(8,128)S(1)}, f32[16,4,8,128]{3,2,1,0:T(8,128)}, u32[]{:S(2)}) copy-start(f32[16,4,8,128]{3,2,1,0:T(8,128)} %param.4) | copy-start | bytes 786436
  0.6 19.2 %copy-start.9 = (f32[3]{0:T(128)S(1)}, f32[3]{0:T(128)}, u32[]{:S(2)}) copy-start(f32[3]{0:T(128)} %param.7) | copy-start | bytes 40
  1.9 9.0 %collective-permute-start.1 = (f32[48,1,8,128]{3,0,2,1:T(8,128)S(1)}, f32[48,1,8,128]{3,0,2,1:T(8,128)S(1)}, u32[]{:S(2)}, u32[]{:S(2)}) collective-permute-start(f32[48,1,8,128]{3,0,2,1:T(8,128)S(1)} %get-tuple-element.82), channel_id=1, source_target_pairs={{0,2},{2,4},{4,6},{6,8},{8,10},{10,12},{12,14},{14,16},{16,18},{18... | collective-permute-start | bytes 589832 | tf_op jit(solution)/shard_map/ppermute | solution.py:17
  6.8 10.3 %collective-permute-start = (f32[48,1,8,128]{3,0,2,1:T(8,128)S(1)}, f32[48,1,8,128]{3,0,2,1:T(8,128)S(1)}, u32[]{:S(2)}, u32[]{:S(2)}) collective-permute-start(f32[48,1,8,128]{3,0,2,1:T(8,128)S(1)} %get-tuple-element.83), channel_id=1, source_target_pairs={{2,0},{4,2},{6,4},{8,6},{10,8},{12,10},{14,12},{16,14},{18,16},{20... | collective-permute-start | bytes 589832 | tf_op jit(solution)/shard_map/ppermute | solution.py:19
  17.1 5.4 copy-start.7
  17.1 3.1 collective-permute-start.3
  18.4 3.3 collective-permute-start.2
  23.1 157.7 %copy-start.2 = (f32[48,4,8,128]{3,0,2,1:T(8,128)}, f32[48,4,8,128]{3,0,2,1:T(8,128)S(1)}, u32[]{:S(2)}) copy-start(f32[48,4,8,128]{3,0,2,1:T(8,128)S(1)} %get-tuple-element.51) | copy-start | bytes 2359300
  63.5 11.6 %collective-permute-start.5 = (f32[48,1,8,128]{3,0,2,1:T(8,128)S(1)}, f32[48,1,8,128]{3,0,2,1:T(8,128)S(1)}, u32[]{:S(2)}, u32[]{:S(2)}) collective-permute-start(f32[48,1,8,128]{3,0,2,1:T(8,128)S(1)} %get-tuple-element.80), channel_id=1, source_target_pairs={{0,2},{2,4},{4,6},{6,8},{8,10},{10,12},{12,14},{14,16},{16,18},{18... | collective-permute-start | bytes 589832 | tf_op jit(solution)/shard_map/ppermute | solution.py:17
  67.7 9.3 %collective-permute-start.4 = (f32[48,1,8,128]{3,0,2,1:T(8,128)S(1)}, f32[48,1,8,128]{3,0,2,1:T(8,128)S(1)}, u32[]{:S(2)}, u32[]{:S(2)}) collective-permute-start(f32[48,1,8,128]{3,0,2,1:T(8,128)S(1)} %get-tuple-element.81), channel_id=1, source_target_pairs={{2,0},{4,2},{6,4},{8,6},{10,8},{12,10},{14,12},{16,14},{18,16},{20... | collective-permute-start | bytes 589832 | tf_op jit(solution)/shard_map/ppermute | solution.py:19
  77.0 2.6 collective-permute-start.7
  78.3 3.3 collective-permute-start.6
  83.2 58.6 %copy-start.5 = (f32[48,4,8,128]{3,0,2,1:T(8,128)}, f32[48,4,8,128]{3,0,2,1:T(8,128)S(1)}, u32[]{:S(2)}) copy-start(f32[48,4,8,128]{3,0,2,1:T(8,128)S(1)} %get-tuple-element.49) | copy-start | bytes 2359300
  122.9 11.6 %collective-permute-start.9 = (f32[48,1,8,128]{3,0,2,1:T(8,128)S(1)}, f32[48,1,8,128]{3,0,2,1:T(8,128)S(1)}, u32[]{:S(2)}, u32[]{:S(2)}) collective-permute-start(f32[48,1,8,128]{3,0,2,1:T(8,128)S(1)} %get-tuple-element.78), channel_id=1, source_target_pairs={{0,2},{2,4},{4,6},{6,8},{8,10},{10,12},{12,14},{14,16},{16,18},{18... | collective-permute-start | bytes 589832 | tf_op jit(solution)/shard_map/ppermute | solution.py:17
  127.1 9.3 %collective-permute-start.8 = (f32[48,1,8,128]{3,0,2,1:T(8,128)S(1)}, f32[48,1,8,128]{3,0,2,1:T(8,128)S(1)}, u32[]{:S(2)}, u32[]{:S(2)}) collective-permute-start(f32[48,1,8,128]{3,0,2,1:T(8,128)S(1)} %get-tuple-element.79), channel_id=1, source_target_pairs={{2,0},{4,2},{6,4},{8,6},{10,8},{12,10},{14,12},{16,14},{18,16},{20... | collective-permute-start | bytes 589832 | tf_op jit(solution)/shard_map/ppermute | solution.py:19
  136.4 2.6 collective-permute-start.11
  137.7 3.3 collective-permute-start.10
  182.2 7.4 %collective-permute-start.13 = (f32[48,1,8,128]{3,0,2,1:T(8,128)S(1)}, f32[48,1,8,128]{3,0,2,1:T(8,128)S(1)}, u32[]{:S(2)}, u32[]{:S(2)}) collective-permute-start(f32[48,1,8,128]{3,0,2,1:T(8,128)S(1)} %get-tuple-element.76), channel_id=1, source_target_pairs={{0,2},{2,4},{4,6},{6,8},{8,10},{10,12},{12,14},{14,16},{16,18},{18... | collective-permute-start | bytes 589832 | tf_op jit(solution)/shard_map/ppermute | solution.py:17
  186.4 9.1 %collective-permute-start.12 = (f32[48,1,8,128]{3,0,2,1:T(8,128)S(1)}, f32[48,1,8,128]{3,0,2,1:T(8,128)S(1)}, u32[]{:S(2)}, u32[]{:S(2)}) collective-permute-start(f32[48,1,8,128]{3,0,2,1:T(8,128)S(1)} %get-tuple-element.77), channel_id=1, source_target_pairs={{2,0},{4,2},{6,4},{8,6},{10,8},{12,10},{14,12},{16,14},{18,16},{20... | collective-permute-start | bytes 589832 | tf_op jit(solution)/shard_map/ppermute | solution.py:19
  195.5 2.6 collective-permute-start.15
  196.8 3.3 collective-permute-start.14
  243.3 11.6 %collective-permute-start.17 = (f32[48,1,8,128]{3,0,2,1:T(8,128)S(1)}, f32[48,1,8,128]{3,0,2,1:T(8,128)S(1)}, u32[]{:S(2)}, u32[]{:S(2)}) collective-permute-start(f32[48,1,8,128]{3,0,2,1:T(8,128)S(1)} %get-tuple-element.74), channel_id=1, source_target_pairs={{0,2},{2,4},{4,6},{6,8},{8,10},{10,12},{12,14},{14,16},{16,18},{18... | collective-permute-start | bytes 589832 | tf_op jit(solution)/shard_map/ppermute | solution.py:17
  247.5 9.3 %collective-permute-start.16 = (f32[48,1,8,128]{3,0,2,1:T(8,128)S(1)}, f32[48,1,8,128]{3,0,2,1:T(8,128)S(1)}, u32[]{:S(2)}, u32[]{:S(2)}) collective-permute-start(f32[48,1,8,128]{3,0,2,1:T(8,128)S(1)} %get-tuple-element.75), channel_id=1, source_target_pairs={{2,0},{4,2},{6,4},{8,6},{10,8},{12,10},{14,12},{16,14},{18,16},{20... | collective-permute-start | bytes 589832 | tf_op jit(solution)/shard_map/ppermute | solution.py:19
  256.8 2.8 collective-permute-start.19
  258.1 3.3 collective-permute-start.18
  303.6 7.4 %collective-permute-start.21 = (f32[48,1,8,128]{3,0,2,1:T(8,128)S(1)}, f32[48,1,8,128]{3,0,2,1:T(8,128)S(1)}, u32[]{:S(2)}, u32[]{:S(2)}) collective-permute-start(f32[48,1,8,128]{3,0,2,1:T(8,128)S(1)} %get-tuple-element.72), channel_id=1, source_target_pairs={{0,2},{2,4},{4,6},{6,8},{8,10},{10,12},{12,14},{14,16},{16,18},{18... | collective-permute-start | bytes 589832 | tf_op jit(solution)/shard_map/ppermute | solution.py:17
  307.8 9.1 %collective-permute-start.20 = (f32[48,1,8,128]{3,0,2,1:T(8,128)S(1)}, f32[48,1,8,128]{3,0,2,1:T(8,128)S(1)}, u32[]{:S(2)}, u32[]{:S(2)}) collective-permute-start(f32[48,1,8,128]{3,0,2,1:T(8,128)S(1)} %get-tuple-element.73), channel_id=1, source_target_pairs={{2,0},{4,2},{6,4},{8,6},{10,8},{12,10},{14,12},{16,14},{18,16},{20... | collective-permute-start | bytes 589832 | tf_op jit(solution)/shard_map/ppermute | solution.py:19
  316.9 2.6 collective-permute-start.23
  318.2 3.3 collective-permute-start.22
  364.9 19.0 %copy-start.3 = (f32[48,4,8,128]{3,0,2,1:T(8,128)}, f32[48,4,8,128]{3,0,2,1:T(8,128)S(1)}, u32[]{:S(2)}) copy-start(f32[48,4,8,128]{3,0,2,1:T(8,128)S(1)} %multiply_add_fusion) | copy-start | bytes 2359300
  364.9 11.6 %collective-permute-start.25 = (f32[48,1,8,128]{3,0,2,1:T(8,128)S(1)}, f32[48,1,8,128]{3,0,2,1:T(8,128)S(1)}, u32[]{:S(2)}, u32[]{:S(2)}) collective-permute-start(f32[48,1,8,128]{3,0,2,1:T(8,128)S(1)} %get-tuple-element.70), channel_id=1, source_target_pairs={{0,2},{2,4},{4,6},{6,8},{8,10},{10,12},{12,14},{14,16},{16,18},{18... | collective-permute-start | bytes 589832 | tf_op jit(solution)/shard_map/ppermute | solution.py:17
  369.1 9.3 %collective-permute-start.24 = (f32[48,1,8,128]{3,0,2,1:T(8,128)S(1)}, f32[48,1,8,128]{3,0,2,1:T(8,128)S(1)}, u32[]{:S(2)}, u32[]{:S(2)}) collective-permute-start(f32[48,1,8,128]{3,0,2,1:T(8,128)S(1)} %get-tuple-element.71), channel_id=1, source_target_pairs={{2,0},{4,2},{6,4},{8,6},{10,8},{12,10},{14,12},{16,14},{18,16},{20... | collective-permute-start | bytes 589832 | tf_op jit(solution)/shard_map/ppermute | solution.py:19
  378.4 2.6 collective-permute-start.27
  379.7 3.3 collective-permute-start.26
  425.2 18.8 %copy-start.4 = (f32[48,4,8,128]{3,0,2,1:T(8,128)}, f32[48,4,8,128]{3,0,2,1:T(8,128)S(1)}, u32[]{:S(2)}) copy-start(f32[48,4,8,128]{3,0,2,1:T(8,128)S(1)} %multiply_subtract_fusion) | copy-start | bytes 2359300
  425.2 7.4 %collective-permute-start.29 = (f32[48,1,8,128]{3,0,2,1:T(8,128)S(1)}, f32[48,1,8,128]{3,0,2,1:T(8,128)S(1)}, u32[]{:S(2)}, u32[]{:S(2)}) collective-permute-start(f32[48,1,8,128]{3,0,2,1:T(8,128)S(1)} %get-tuple-element.68), channel_id=1, source_target_pairs={{0,2},{2,4},{4,6},{6,8},{8,10},{10,12},{12,14},{14,16},{16,18},{18... | collective-permute-start | bytes 589832 | tf_op jit(solution)/shard_map/ppermute | solution.py:17
  429.4 9.1 %collective-permute-start.28 = (f32[48,1,8,128]{3,0,2,1:T(8,128)S(1)}, f32[48,1,8,128]{3,0,2,1:T(8,128)S(1)}, u32[]{:S(2)}, u32[]{:S(2)}) collective-permute-start(f32[48,1,8,128]{3,0,2,1:T(8,128)S(1)} %get-tuple-element.69), channel_id=1, source_target_pairs={{2,0},{4,2},{6,4},{8,6},{10,8},{12,10},{14,12},{16,14},{18,16},{20... | collective-permute-start | bytes 589832 | tf_op jit(solution)/shard_map/ppermute | solution.py:19
  438.5 2.6 collective-permute-start.31
  439.8 3.3 collective-permute-start.30
  484.0 2.9 copy-start
  572.5 7.3 %copy-start.1 = (f32[256,4,8,128]{3,2,1,0:T(8,128)S(1)}, f32[256,4,8,128]{3,2,1,0:T(8,128)}, u32[]{:S(2)}) copy-start(f32[256,4,8,128]{3,2,1,0:T(8,128)} %param.5) | copy-start | bytes 12582916
  671.6 1.2 copy-start.8
